TPU v7x, 128 devices: a whole 4x4x4 slice. The times are simulated.
128 devices in a mesh: sector: 64 (over x, y, z_lo, core), dof: 2 (over z_hi).
Axes of the slice: x: 4, y: 4, z: 4 (z_hi: 2, z_lo: 2; z = z_hi * 2 + z_lo), core: 2. Of those that a mesh axis runs over, the one named last changes fastest.
Arguments:
- loads: bfloat16 [64, 128, 32768], P('sector', None, 'dof'), may hold values from -0.75 to 0.75
- modes: bfloat16 [32768, 512], P('dof'), may hold values from -0.25 to 0.25
- response: float32 [64, 128, 512], P('sector', None, 'dof'), may hold values from -6 to 6
- pattern: int32 [64], P('sector'), may hold values from 0 to 7
- deviation: float32 [8, 512], replicated, may hold values from -1 to 1
- eigen: float32 [64, 512], replicated, may hold values from 1 to 10
- loss: float32 [512], replicated, may hold values from 0.2 to 0.6
- omega_sq: float32 [64], replicated, may hold values from 0.5 to 12
- iface_left: int32 [1024], P('dof'), may hold values from 0 to 16383, as said below
- iface_right: int32 [1024], P('dof'), may hold values from 0 to 16383, as said below
Outputs:
- modal_response: float32 [64, 128, 512], P('sector', None, 'dof')
- displacement: bfloat16 [64, 128, 32768], P('sector', None, 'dof')
Inputs may be any that keep to these rules, and one draw needn't show every extreme that they name: Within each block of 512 entries, the entries of iface_left and of iface_right together are (2) * 512 distinct rows. `iface_right`: see iface_left.
All inputs are finite; a program needn't handle non-finite values.
Results may differ from a plain program's by a relative error of at most 0.005.
Values may be sent and summed in bfloat16 or wider, within the bound.
No kernel may reach another device: no remote copies, remote signals or barrier semaphores. Data moves between devices by JAX's collectives and lax.ppermute only.
A program may use at most 128 MiB of HBM per device.

v0:
```python
import functools
import math

import jax
import jax.numpy as jnp
import numpy as np
from jax import lax
from jax.experimental import pallas as pl
from jax.experimental.pallas import tpu as pltpu
from jax.sharding import Mesh
from jax.sharding import PartitionSpec as P

SECTOR = ("sector_0", "sector_1", "sector_2", "sector_3")
EVERY = SECTOR + ("dof",)
BF16 = jnp.bfloat16
F32 = jnp.float32
EMPTY = 3.0e38
NEAR = 3


def split_bf16(table):
    high = table.astype(np.float32).astype(jnp.bfloat16)
    low = (table - high.astype(np.float64)).astype(np.float32).astype(jnp.bfloat16)
    return high, low


def transforms(sectors, dofs):
    turns = np.outer(np.arange(sectors), np.arange(sectors)) % sectors
    theta = turns * (2.0 * math.pi / sectors)
    cosine, sine = np.cos(theta), np.sin(theta)
    forward = np.zeros((2, sectors, sectors, dofs, 2))
    for d in range(dofs):
        forward[0, :, :, d, 0] = cosine
        forward[0, :, :, d, 1] = sine
        forward[1, :, :, d, 0] = -sine
        forward[1, :, :, d, 1] = cosine
    forward = forward.reshape(2 * sectors, sectors * dofs * 2)
    inverse = np.zeros((sectors, 2, 2, sectors))
    inverse[:, 0, 0, :] = cosine / sectors
    inverse[:, 0, 1, :] = -sine / sectors
    inverse[:, 1, 0, :] = sine / sectors
    inverse[:, 1, 1, :] = cosine / sectors
    inverse = inverse.reshape(2 * sectors, 2 * sectors)
    return split_bf16(forward), split_bf16(inverse)


def pick(sources, columns):
    sources = np.asarray(sources).reshape(-1)
    out = np.zeros((sources.size, columns), np.float32)
    out[np.arange(sources.size), sources] = 1.0
    return out.astype(jnp.bfloat16)


def send_order(freqs):
    f, side, part = np.meshgrid(np.arange(freqs), np.arange(2), np.arange(2), indexing="ij")
    return pick((side * 2 + part) * freqs + f, 4 * freqs)


def back_order(sectors, dofs):
    s, _, part, lanes = np.meshgrid(
        np.arange(sectors), np.arange(dofs), np.arange(2), np.arange(2), indexing="ij"
    )
    return pick(lanes * 2 * sectors + s * 2 + part, 4 * sectors)


def seen_order(few):
    side, lanes, part, f = np.meshgrid(
        np.arange(2), np.arange(2), np.arange(2), np.arange(few), indexing="ij"
    )
    return pick(((f * 2 + side) * 2 + part) * 2 + lanes, 8 * few)


def dot(a, b):
    return jnp.dot(a, b, preferred_element_type=F32)


def dot_t(a, b):
    return lax.dot_general(a, b, (((1,), (1,)), ((), ())), preferred_element_type=F32)


def part_of(start, size):
    return pl.ds(pl.multiple_of(start * size, size), size)


def within(array, space):
    return pltpu.with_memory_space_constraint(array, space)


def params(mib):
    return pltpu.CompilerParams(vmem_limit_bytes=mib << 20)


AHEAD = 6
SLOTS = 8
GROUP = 32
ROWS = 8


def gather_rows(index, held, near, first_out):
    row = lax.broadcasted_iota(jnp.int32, (8, 128), 0)
    shape = (GROUP, GROUP * ROWS)
    lane = lax.broadcasted_iota(jnp.int32, shape, 1) - ROWS * lax.broadcasted_iota(
        jnp.int32, shape, 0
    )
    width = held.shape[2]
    for first in range(0, index.shape[0], GROUP):
        blocks, places = [], []
        for j in range(GROUP):
            if j % 8 == 0:
                at = jnp.zeros((8, 128), jnp.int32)
            entry = index[first + j]
            blocks.append(held[lax.shift_right_logical(entry, 3)])
            at = jnp.where(row == j % 8, entry, at)
            if j % 8 == 7:
                places.append(at & (ROWS - 1))
        at = jnp.concatenate(places, 0)
        at = jnp.concatenate([at] * (GROUP * ROWS // 128), 1)
        order = jnp.where(lane == at, 1.0, 0.0).astype(BF16)
        chosen = dot(order, jnp.stack(blocks, 0).reshape(GROUP * ROWS, width)).astype(BF16)
        near[first_out + first : first_out + first + GROUP, :] = chosen


def force_kernel(
    pattern, loads, modes, response, deviation, order, left_in, right_in,
    out, turned, near, spread,
    held, brought, total, acted, table, sorter, left, right,
    load_sems, mode_sems, other_sems
):
    width = modes.shape[2]
    depth = modes.shape[0] * ROWS
    block = depth // mode_sems.shape[0]
    steps = depth // block
    others = [
        pltpu.make_async_copy(response, acted, other_sems.at[0]),
        pltpu.make_async_copy(deviation, table, other_sems.at[1]),
        pltpu.make_async_copy(order, sorter, other_sems.at[2]),
        pltpu.make_async_copy(left_in, left, other_sems.at[3]),
        pltpu.make_async_copy(right_in, right, other_sems.at[4]),
    ]

    def copies(k):
        cut = part_of(k, block)
        blocks = part_of(k, block // ROWS)
        return (
            pltpu.make_async_copy(modes.at[blocks], held.at[blocks], mode_sems.at[k]),
            pltpu.make_async_copy(
                loads.at[:, cut], brought.at[lax.rem(k, SLOTS)], load_sems.at[k]
            ),
        )

    for k in range(AHEAD):
        for c in copies(k):
            c.start()
    for c in others:
        c.start()
    total[...] = jnp.zeros_like(total)
    size = 256

    def step(k, carry):
        for c in copies(k):
            c.wait()

        @pl.when(k + AHEAD < steps)
        def _():
            for c in copies(k + AHEAD):
                c.start()

        blocks = held[part_of(k, block // ROWS)].reshape(block, width)
        total[...] += dot(brought[lax.rem(k, SLOTS)], blocks)
        for j in range(block // size):
            here = part_of(k * (block // size) + j, size)
            turned[:, here] = held[part_of(k * (block // size) + j, size // ROWS)].reshape(size, width).T
            spread[here, :] = jnp.full((size, spread.shape[1]), EMPTY, F32)
        return carry

    lax.fori_loop(0, steps, step, 0)
    for c in others:
        c.wait()
    half = acted.shape[1]
    mine = part_of(lax.axis_index("dof"), half)
    total[:, mine] -= table[pl.ds(pattern[0], 1), mine] * acted[...]
    stacked = jnp.concatenate([total[:, :half], total[:, half:]], 0).astype(BF16)
    out[...] = dot(sorter[...], stacked).astype(BF16).reshape(out.shape)
    gather_rows(left, held, near, 0)
    gather_rows(right, held, near, left.shape[0])


def force(loads, modes, response, pattern, deviation, order, left, right):
    rows, depth = loads.shape
    width = modes.shape[1]
    half = response.shape[1]
    steps = 16
    entries = left.shape[0]
    vmem = pl.BlockSpec(memory_space=pltpu.VMEM)
    hbm = pl.BlockSpec(memory_space=pltpu.HBM)
    args = (loads, modes.reshape(depth // ROWS, ROWS, width), response, deviation, order, left, right)
    args = [within(a, pltpu.HBM) for a in args]
    return pl.pallas_call(
        force_kernel,
        out_shape=(
            pltpu.VMEM((rows, 2, half), BF16),
            pltpu.VMEM((width, depth), BF16),
            pltpu.VMEM((2 * entries, width), BF16),
            pltpu.VMEM((depth, rows), F32),
        ),
        in_specs=[pl.BlockSpec(memory_space=pltpu.SMEM)] + [hbm] * len(args),
        out_specs=(vmem,) * 4,
        scratch_shapes=[
            pltpu.VMEM((depth // ROWS, ROWS, width), BF16),
            pltpu.VMEM((SLOTS, rows, depth // steps), BF16),
            pltpu.VMEM((rows, width), F32),
            pltpu.VMEM((rows, half), F32),
            pltpu.VMEM(deviation.shape, F32),
            pltpu.VMEM(order.shape, BF16),
            pltpu.SMEM((entries,), jnp.int32),
            pltpu.SMEM((entries,), jnp.int32),
            pltpu.SemaphoreType.DMA((steps,)),
            pltpu.SemaphoreType.DMA((steps,)),
            pltpu.SemaphoreType.DMA((6,)),
        ],
        compiler_params=params(21),
        cost_estimate=pl.CostEstimate(
            flops=2 * rows * depth * width, bytes_accessed=2 * depth * (rows + width), transcendentals=0
        ),
        name="force",
    )(pattern, *args)


def split_here(value):
    high = value.astype(BF16)
    return high, (value - high.astype(F32)).astype(BF16)


def solve_kernel(omega_sq, got, fwd_hi, fwd_lo, inv_hi, inv_lo, order, eigen, loss, out):
    sectors = eigen.shape[0]
    half = got.shape[-1]
    me = lax.axis_index(EVERY)
    side, freq = me % 2, me // 2
    rows = got[...].reshape(-1, half)
    spec = dot(fwd_hi[...], rows) + dot(fwd_lo[...], rows)
    p, q = spec[:sectors], spec[sectors:]
    mine = part_of(side, half)
    stiff = eigen[:, mine]
    a = stiff - omega_sq[freq]
    b = loss[:, mine] * stiff
    denom = a * a + b * b
    solved = jnp.concatenate([(p * a + q * b) / denom, (q * a - p * b) / denom], 0)
    high, low = split_here(solved)
    own = dot(inv_hi[...], high) + (dot(inv_hi[...], low) + dot(inv_lo[...], high))
    before = jnp.concatenate([own[-2:], own[:-2]], 0)
    after = jnp.concatenate([own[2:], own[:2]], 0)
    lanes = half // 2
    near = jnp.concatenate(
        [jnp.concatenate([v[:, :lanes], v[:, lanes:]], 0) for v in (before, own, after)], 1
    ).astype(BF16)
    out[...] = dot(order[...], near).astype(BF16).reshape(out.shape)


def solve(got, fwd, inv, order, eigen, loss, omega_sq):
    sectors = eigen.shape[0]
    devices, _, half = got.shape
    vmem = pl.BlockSpec(memory_space=pltpu.VMEM)
    args = (got, *fwd, *inv, order, eigen, loss)
    return pl.pallas_call(
        solve_kernel,
        out_shape=pltpu.VMEM((devices, 4, NEAR * half // 2), BF16),
        in_specs=[pl.BlockSpec(memory_space=pltpu.SMEM)] + [vmem] * len(args),
        out_specs=vmem,
        compiler_params=params(6),
        name="solve",
    )(omega_sq, *args)


PHASES = (6144, 4096, 4096, 2048)


def weave(main, side):
    done = 0
    for i, item in enumerate(main):
        item()
        upto = len(side) * (i + 1) // len(main)
        for other in side[done:upto]:
            other()
        done = upto
    for other in side[done:]:
        other()


def recover_kernel(
    left_in, right_in, got, order, near, turned, spread_in, modal, shown, spread,
    resp, fresh, mine_out, left, right, out_sems, other_sems, *raws
):
    width, depth = turned.shape
    rows = spread.shape[1]
    half = width // 2
    freqs = rows // 2
    entries = left.shape[0]
    lanes = half // 2
    few = order.shape[0] // 8
    indexes = [
        pltpu.make_async_copy(left_in, left, other_sems.at[1]),
        pltpu.make_async_copy(right_in, right, other_sems.at[2]),
    ]
    for c in indexes:
        c.start()
    for t in range(freqs // few):
        part = got[2 * few * t : 2 * few * (t + 1)].reshape(8 * few, NEAR * lanes)
        part = dot(order[...], part).astype(BF16)
        for side in range(2):
            for lane in range(2):
                for p in range(2):
                    at = ((side * 2 + lane) * 2 + p) * few
                    for k in range(NEAR):
                        resp[
                            k * rows + p * freqs + t * few : k * rows + p * freqs + (t + 1) * few,
                            side * half + lane * lanes : side * half + (lane + 1) * lanes,
                        ] = part[at : at + few, k * lanes : (k + 1) * lanes]
    mine = part_of(lax.axis_index("dof"), half)
    mine_out[...] = resp[rows : 2 * rows, mine].astype(F32)
    modal_copy = pltpu.make_async_copy(mine_out, modal, other_sems.at[0])
    modal_copy.start()

    at_right = dot_t(near[entries:, :], resp[: 2 * rows, :]).astype(BF16).astype(F32)
    at_left = dot_t(near[:entries, :], resp[rows:, :]).astype(BF16).astype(F32)
    new = 0.5 * (at_right + at_left)
    fresh[:entries, :] = new[:, :rows]
    fresh[entries:, :] = new[:, rows:]

    for c in indexes:
        c.wait()
    size = 256

    def product(at, buffer, cut):
        def run():
            own = resp[rows : 2 * rows, :]
            buffer[:, cut : cut + size] = dot(own, turned[:, at : at + size]).astype(BF16)

        return run

    def scatter(first, count):
        def run():
            for e in range(first, first + count):
                spread[pl.ds(left[e], 1), :] = fresh[e : e + 1, :]
                spread[pl.ds(right[e], 1), :] = fresh[entries + e : entries + e + 1, :]

        return run

    def select(at, buffer, cut):
        def run():
            here = spread[at : at + size, :].astype(BF16).T
            buffer[:, cut : cut + size] = jnp.where(here < 1e38, here, buffer[:, cut : cut + size])

        return run

    starts = [sum(PHASES[:i]) for i in range(len(PHASES))]
    copies = []

    def finish(i):
        span = PHASES[i]
        part = raws[i]
        copy = pltpu.make_async_copy(
            part, shown.at[:, starts[i] : starts[i] + span], out_sems.at[i]
        )
        copy.start()
        copies.append(copy)

    few = 16
    side = [scatter(first, few) for first in range(0, entries, few)]
    for i, span in enumerate(PHASES):
        main = [product(starts[i] + c, raws[i], c) for c in range(0, span, size)]
        weave(main, side)
        if i:
            finish(i - 1)
        side = [select(starts[i] + c, raws[i], c) for c in range(0, span, size)]
    weave([], side)
    finish(len(PHASES) - 1)
    for c in copies:
        c.wait()
    modal_copy.wait()


def recover(got, order, near, turned, spread, left, right):
    width, depth = turned.shape
    rows = spread.shape[1]
    half = width // 2
    entries = left.shape[0]
    vmem = pl.BlockSpec(memory_space=pltpu.VMEM)
    hbm = pl.BlockSpec(memory_space=pltpu.HBM)
    modal, shown, _ = pl.pallas_call(
        recover_kernel,
        out_shape=(
            pltpu.HBM((rows, half), F32),
            pltpu.HBM((rows, depth), BF16),
            pltpu.VMEM(spread.shape, F32),
        ),
        in_specs=[hbm, hbm] + [vmem] * 5,
        out_specs=(hbm, hbm, vmem),
        input_output_aliases={6: 2},
        scratch_shapes=[
            pltpu.VMEM((NEAR * rows, width), BF16),
            pltpu.VMEM((2 * entries, rows), F32),
            pltpu.VMEM((rows, half), F32),
            pltpu.SMEM((entries,), jnp.int32),
            pltpu.SMEM((entries,), jnp.int32),
            pltpu.SemaphoreType.DMA((len(PHASES),)),
            pltpu.SemaphoreType.DMA((3,)),
            *[pltpu.VMEM((rows, span), BF16) for span in PHASES],
        ],
        compiler_params=params(10),
        name="recover",
    )(
        within(left, pltpu.HBM), within(right, pltpu.HBM), got, order, within(near, pltpu.VMEM), within(turned, pltpu.VMEM),
        within(spread, pltpu.VMEM)
    )
    return modal, shown


def exchange(pieces):
    return lax.all_to_all(pieces, EVERY, 0, 0, tiled=True)


def shards(
    loads, modes, response, pattern, deviation, eigen, loss, omega_sq, iface_left, iface_right
):
    rows = loads.shape[1]
    freqs = rows // 2
    sectors = lax.axis_size(SECTOR)
    dofs = lax.axis_size("dof")
    fwd, inv = transforms(sectors, dofs)
    sent, turned, near, spread = force(
        loads[0], modes, response[0], pattern, deviation, send_order(freqs), iface_left, iface_right
    )
    got = exchange(sent)
    back = solve(got, fwd, inv, back_order(sectors, dofs), eigen, loss[None], omega_sq)
    seen = exchange(back)
    modal, shown = recover(seen, seen_order(32), near, turned, spread, iface_left, iface_right)
    return modal[None], shown[None]


def solution(mesh):
    torus = Mesh(
        mesh.devices.reshape(4, 4, 2, 2, mesh.shape["dof"]),
        ("sector_0", "sector_1", "sector_2", "sector_3", "dof"),
    )
    return jax.shard_map(
        shards,
        mesh=torus,
        in_specs=(
            P(SECTOR, None, "dof"),
            P("dof", None),
            P(SECTOR, None, "dof"),
            P(SECTOR),
            P(),
            P(),
            P(),
            P(),
            P("dof"),
            P("dof"),
        ),
        out_specs=(P(SECTOR, None, "dof"), P(SECTOR, None, "dof")),
        check_vma=False,
    )
```

profile of v0, /device:TPU:1, one launch (start us, length us, event | category | flops | bytes accessed | tf_op | source)
XLA Modules:
  0.0 56.4 jit_solution(14453219768624840258)
XLA Ops:
  1.3 0.0 copy-start
  1.3 0.0 copy-start.2
  1.3 0.0 copy-start.3
  1.3 0.0 copy-start.4
  1.3 0.0 copy-start.5
  1.3 0.0 copy-start.6
  1.4 0.0 copy-start.7
  1.4 0.0 copy-start.8
  1.4 0.0 copy-start.1
  1.4 9.9 %force.1 = (bf16[128,2,256]{2,1,0:T(2,128)(2,1)S(1)}, bf16[512,16384]{1,0:T(8,128)(2,1)S(1)}, bf16[1024,512]{1,0:T(8,128)(2,1)S(1)}, f32[16384,128]{1,0:T(8,128)S(1)}) custom-call(s32[1]{0:T(128)S(6)} %copy.21.pattern, bf16[128,16384]{1,0:T(8,128)(2,1)} %bitcast.8, bf16[2048,8,512]{2,1,0:T(8,128)(2,1)} %bitcast.7, f32[128,256]{1,0:T(8,128)} %bitcast.9, ...), custom_call_target="tpu_custom_call" | custom-call | flops 2147483648 | bytes 20971520 | tf_op jit(solution)/shard_map/force/pallas_call | solution.py:198
  11.3 21.4 %all_to_all.10.got = bf16[128,2,256]{2,1,0:T(2,128)(2,1)S(1)} all-to-all(bf16[128,2,256]{2,1,0:T(2,128)(2,1)S(1)} %get-tuple-element.8), channel_id=1, replica_groups=mesh['sector_0'=4,'sector_1'=4,'sector_2'=2,'sector_3'=2,'dof'=2] {'sect..., dimensions={0} | all-to-all | bytes 262144 | tf_op jit(solution)/shard_map/all_to_all | solution.py:419
  32.7 0.0 copy-done
  32.7 0.0 copy-done.2
  32.7 0.0 copy-done.3
  32.7 0.0 copy-done.4
  32.7 0.0 copy-done.5
  32.7 0.0 copy-done.6
  32.8 0.0 copy-done.7
  32.8 0.0 copy-done.8
  32.8 1.3 %solve.1 = bf16[128,4,384]{2,1,0:T(4,128)(2,1)S(1)} custom-call(f32[64]{0:T(128)S(1)} %copy-done.8, bf16[128,2,256]{2,1,0:T(2,128)(2,1)S(1)} %all_to_all.10.got, bf16[128,256]{1,0:T(8,128)(2,1)S(1)} %copy-done.4, bf16[128,256]{1,0:T(8,128)(2,1)S(1)} %copy-done.3, bf16[128,128]{1,0:T(8,128)(2,1)S(1)} %copy-done.6, bf16[128,128]{1,0:T(8,128)(2,1)S(1)} %copy-done.5, ...), custom_call_target="tpu_custom_call" | custom-call | tf_op jit(solution)/shard_map/solve/pallas_call | solution.py:264
  34.1 16.3 %all_to_all.11.got = bf16[128,4,384]{2,1,0:T(4,128)(2,1)S(1)} all-to-all(bf16[128,4,384]{2,1,0:T(4,128)(2,1)S(1)} %solve.1), channel_id=1, replica_groups=mesh['sector_0'=4,'sector_1'=4,'sector_2'=2,'sector_3'=2,'dof'=2] {'sect..., dimensions={0} | all-to-all | bytes 786432 | tf_op jit(solution)/shard_map/all_to_all | solution.py:419
  50.3 0.0 copy-done.1
  50.3 6.1 %recover.1 = (f32[128,256]{1,0:T(8,128)}, bf16[128,16384]{1,0:T(8,128)(2,1)}, f32[16384,128]{1,0:T(8,128)S(1)}) custom-call(s32[512]{0:T(512)} %left_in.3, s32[512]{0:T(512)} %right_in.3, bf16[128,4,384]{2,1,0:T(4,128)(2,1)S(1)} %all_to_all.11.got, bf16[256,256]{1,0:T(8,128)(2,1)S(1)} %copy-done.1, ...), custom_call_target="tpu_custom_call", output_to_operand_aliasing={{2}: (6, {})} | custom-call | tf_op jit(solution)/shard_map/recover/pallas_call | solution.py:389
Async XLA Ops:
  1.3 31.4 %copy-start = (bf16[512,256]{1,0:T(8,128)(2,1)S(1)}, bf16[512,256]{1,0:T(8,128)(2,1)}, u32[]{:S(2)}) copy-start(bf16[512,256]{1,0:T(8,128)(2,1)} %constant.19.clone.order) | copy-start | bytes 786436
  1.3 31.4 %copy-start.2 = (f32[64,512]{1,0:T(8,128)S(1)}, f32[64,512]{1,0:T(8,128)}, u32[]{:S(2)}) copy-start(f32[64,512]{1,0:T(8,128)} %eigen.1) | copy-start | bytes 393220
  1.3 31.4 %copy-start.3 = (bf16[128,256]{1,0:T(8,128)(2,1)S(1)}, bf16[128,256]{1,0:T(8,128)(2,1)}, u32[]{:S(2)}) copy-start(bf16[128,256]{1,0:T(8,128)(2,1)} %constant.16.clone.fwd_lo) | copy-start | bytes 196612
  1.3 31.4 %copy-start.4 = (bf16[128,256]{1,0:T(8,128)(2,1)S(1)}, bf16[128,256]{1,0:T(8,128)(2,1)}, u32[]{:S(2)}) copy-start(bf16[128,256]{1,0:T(8,128)(2,1)} %constant.15.clone.fwd_hi) | copy-start | bytes 196612
  1.3 31.4 %copy-start.5 = (bf16[128,128]{1,0:T(8,128)(2,1)S(1)}, bf16[128,128]{1,0:T(8,128)(2,1)}, u32[]{:S(2)}) copy-start(bf16[128,128]{1,0:T(8,128)(2,1)} %constant.18.clone.inv_lo) | copy-start | bytes 98308
  1.3 31.4 %copy-start.6 = (bf16[128,128]{1,0:T(8,128)(2,1)S(1)}, bf16[128,128]{1,0:T(8,128)(2,1)}, u32[]{:S(2)}) copy-start(bf16[128,128]{1,0:T(8,128)(2,1)} %constant.17.clone.inv_hi) | copy-start | bytes 98308
  1.4 31.4 %copy-start.7 = (f32[512]{0:T(512)S(1)}, f32[512]{0:T(512)}, u32[]{:S(2)}) copy-start(f32[512]{0:T(512)} %param.23) | copy-start | bytes 6148
  1.4 31.4 %copy-start.8 = (f32[64]{0:T(128)S(1)}, f32[64]{0:T(128)}, u32[]{:S(2)}) copy-start(f32[64]{0:T(128)} %omega_sq.1) | copy-start | bytes 772
  1.4 49.0 %copy-start.1 = (bf16[256,256]{1,0:T(8,128)(2,1)S(1)}, bf16[256,256]{1,0:T(8,128)(2,1)}, u32[]{:S(2)}) copy-start(bf16[256,256]{1,0:T(8,128)(2,1)} %constant.20.clone.order) | copy-start | bytes 393220
where the time goes:
time: 56.6 us; the launch traced here: 56.4 us
  blocking collectives  37.7 us (67%)
  Pallas kernels  17.3 us (31%)
  between operations  1.41 us (2%)
    all_to_all x2, blocking collectives, exchange(): return lax.all_to_all(pieces, EVERY, 0, 0, tiled=True)  37.7 us
    pallas_call x1, Pallas kernels, force(): pl.pallas_call(force_kernel, out_shape=(pltpu.VMEM((rows, 2, half), BF16)...  9.89 us
    pallas_call x1, Pallas kernels, recover(): pl.pallas_call(recover_kernel, out_shape=(pltpu.HBM((rows, half), F32), p...  6.07 us
    pallas_call x1, Pallas kernels, solve(): pl.pallas_call(solve_kernel, out_shape=pltpu.VMEM((devices, 4, NEAR * hal...  1.3 us

commit v1 on v0

--- a/solution.py
+++ b/solution.py
@@ -231,7 +231,7 @@
     return high, (value - high.astype(F32)).astype(BF16)
 
 
-def solve_kernel(omega_sq, got, fwd_hi, fwd_lo, inv_hi, inv_lo, order, eigen, loss, out):
+def solve_kernel(got, fwd_hi, fwd_lo, inv_hi, inv_lo, order, eigen, loss, omega_sq, out):
     sectors = eigen.shape[0]
     half = got.shape[-1]
     me = lax.axis_index(EVERY)
@@ -241,7 +241,8 @@
     p, q = spec[:sectors], spec[sectors:]
     mine = part_of(side, half)
     stiff = eigen[:, mine]
-    a = stiff - omega_sq[freq]
+    at = lax.broadcasted_iota(jnp.int32, omega_sq.shape, 1) == freq
+    a = stiff - jnp.sum(jnp.where(at, omega_sq[...], 0.0), axis=1, keepdims=True)
     b = loss[:, mine] * stiff
     denom = a * a + b * b
     solved = jnp.concatenate([(p * a + q * b) / denom, (q * a - p * b) / denom], 0)
@@ -260,18 +261,19 @@
     sectors = eigen.shape[0]
     devices, _, half = got.shape
     vmem = pl.BlockSpec(memory_space=pltpu.VMEM)
-    args = (got, *fwd, *inv, order, eigen, loss)
+    args = (got, *fwd, *inv, order, eigen, loss, omega_sq)
     return pl.pallas_call(
         solve_kernel,
         out_shape=pltpu.VMEM((devices, 4, NEAR * half // 2), BF16),
-        in_specs=[pl.BlockSpec(memory_space=pltpu.SMEM)] + [vmem] * len(args),
+        in_specs=[vmem] * len(args),
         out_specs=vmem,
         compiler_params=params(6),
         name="solve",
-    )(omega_sq, *args)
+    )(*args)
 
 
 PHASES = (6144, 4096, 4096, 2048)
+PIECE = 1024
 
 
 def weave(main, side):
@@ -355,25 +357,30 @@
     starts = [sum(PHASES[:i]) for i in range(len(PHASES))]
     copies = []
 
-    def finish(i):
-        span = PHASES[i]
-        part = raws[i]
-        copy = pltpu.make_async_copy(
-            part, shown.at[:, starts[i] : starts[i] + span], out_sems.at[i]
-        )
-        copy.start()
-        copies.append(copy)
+    def send(i, cut):
+        def run():
+            at = starts[i] + cut
+            copy = pltpu.make_async_copy(
+                raws[i].at[:, cut : cut + PIECE],
+                shown.at[:, at : at + PIECE],
+                out_sems.at[at // PIECE],
+            )
+            copy.start()
+            copies.append(copy)
+
+        return run
 
     few = 16
     side = [scatter(first, few) for first in range(0, entries, few)]
     for i, span in enumerate(PHASES):
         main = [product(starts[i] + c, raws[i], c) for c in range(0, span, size)]
         weave(main, side)
-        if i:
-            finish(i - 1)
-        side = [select(starts[i] + c, raws[i], c) for c in range(0, span, size)]
+        side = []
+        for c in range(0, span, size):
+            side.append(select(starts[i] + c, raws[i], c))
+            if (c + size) % PIECE == 0:
+                side.append(send(i, c + size - PIECE))
     weave([], side)
-    finish(len(PHASES) - 1)
     for c in copies:
         c.wait()
     modal_copy.wait()
@@ -393,7 +400,7 @@
             pltpu.HBM((rows, depth), BF16),
             pltpu.VMEM(spread.shape, F32),
         ),
-        in_specs=[hbm, hbm] + [vmem] * 5,
+        in_specs=[vmem] * 7,
         out_specs=(hbm, hbm, vmem),
         input_output_aliases={6: 2},
         scratch_shapes=[
@@ -402,14 +409,14 @@
             pltpu.VMEM((rows, half), F32),
             pltpu.SMEM((entries,), jnp.int32),
             pltpu.SMEM((entries,), jnp.int32),
-            pltpu.SemaphoreType.DMA((len(PHASES),)),
+            pltpu.SemaphoreType.DMA((depth // PIECE,)),
             pltpu.SemaphoreType.DMA((3,)),
             *[pltpu.VMEM((rows, span), BF16) for span in PHASES],
         ],
         compiler_params=params(10),
         name="recover",
     )(
-        within(left, pltpu.HBM), within(right, pltpu.HBM), got, order, within(near, pltpu.VMEM), within(turned, pltpu.VMEM),
+        left, right, got, order, within(near, pltpu.VMEM), within(turned, pltpu.VMEM),
         within(spread, pltpu.VMEM)
     )
     return modal, shown
@@ -431,7 +438,7 @@
         loads[0], modes, response[0], pattern, deviation, send_order(freqs), iface_left, iface_right
     )
     got = exchange(sent)
-    back = solve(got, fwd, inv, back_order(sectors, dofs), eigen, loss[None], omega_sq)
+    back = solve(got, fwd, inv, back_order(sectors, dofs), eigen, loss[None], omega_sq[None])
     seen = exchange(back)
     modal, shown = recover(seen, seen_order(32), near, turned, spread, iface_left, iface_right)
     return modal[None], shown[None]

time: 56.6 us -> 55.2 us (0.975)
  Pallas kernels: 17.3 us -> 15.8 us
    pallas_call x1, Pallas kernels: 6.07 us -> 5.15 us  [recover(): pl.pallas_call(recover_kernel, out_shape=(pltpu.HBM((rows, half), F32), p...]
where the time goes in v1:
time: 55.2 us; the launch traced here: 55 us
  blocking collectives  37.7 us (68%)
  Pallas kernels  15.8 us (29%)
  between operations  1.43 us (3%)
    all_to_all x2, blocking collectives, exchange(): return lax.all_to_all(pieces, EVERY, 0, 0, tiled=True)  37.7 us
    pallas_call x1, Pallas kernels, force(): pl.pallas_call(force_kernel, out_shape=(pltpu.VMEM((rows, 2, half), BF16)...  9.93 us
    pallas_call x1, Pallas kernels, recover(): pl.pallas_call(recover_kernel, out_shape=(pltpu.HBM((rows, half), F32), p...  5.15 us

profile of v1, /device:TPU:1, one launch (start us, length us, event | category | flops | bytes accessed | tf_op | source)
XLA Modules:
  0.0 55.0 jit_solution(3440333816295212008)
XLA Ops:
  1.3 0.0 copy-start
  1.3 0.0 copy-start.2
  1.3 0.0 copy-start.3
  1.3 0.0 copy-start.4
  1.3 0.0 copy-start.5
  1.3 0.0 copy-start.6
  1.4 0.0 copy-start.9
  1.4 0.0 copy-start.10
  1.4 0.0 copy-start.1
  1.4 0.0 copy-start.7
  1.4 0.0 copy-start.8
  1.4 9.9 %force.1 = (bf16[128,2,256]{2,1,0:T(2,128)(2,1)S(1)}, bf16[512,16384]{1,0:T(8,128)(2,1)S(1)}, bf16[1024,512]{1,0:T(8,128)(2,1)S(1)}, f32[16384,128]{1,0:T(8,128)S(1)}) custom-call(s32[1]{0:T(128)S(6)} %copy.21.pattern, bf16[128,16384]{1,0:T(8,128)(2,1)} %bitcast.10, bf16[2048,8,512]{2,1,0:T(8,128)(2,1)} %bitcast.9, f32[128,256]{1,0:T(8,128)} %bitcast.11, ...), custom_call_target="tpu_custom_call" | custom-call | flops 2147483648 | bytes 20971520 | tf_op jit(solution)/shard_map/force/pallas_call | solution.py:198
  11.3 21.4 %all_to_all.10.got = bf16[128,2,256]{2,1,0:T(2,128)(2,1)S(1)} all-to-all(bf16[128,2,256]{2,1,0:T(2,128)(2,1)S(1)} %get-tuple-element.8), channel_id=1, replica_groups=mesh['sector_0'=4,'sector_1'=4,'sector_2'=2,'sector_3'=2,'dof'=2] {'sect..., dimensions={0} | all-to-all | bytes 262144 | tf_op jit(solution)/shard_map/all_to_all | solution.py:426
  32.8 0.0 copy-done
  32.8 0.0 copy-done.2
  32.8 0.0 copy-done.3
  32.8 0.0 copy-done.4
  32.8 0.0 copy-done.5
  32.8 0.0 copy-done.6
  32.8 0.0 copy-done.9
  32.8 0.8 %solve.1 = bf16[128,4,384]{2,1,0:T(4,128)(2,1)S(1)} custom-call(bf16[128,2,256]{2,1,0:T(2,128)(2,1)S(1)} %all_to_all.10.got, bf16[128,256]{1,0:T(8,128)(2,1)S(1)} %copy-done.4, bf16[128,256]{1,0:T(8,128)(2,1)S(1)} %copy-done.3, bf16[128,128]{1,0:T(8,128)(2,1)S(1)} %copy-done.6, bf16[128,128]{1,0:T(8,128)(2,1)S(1)} %copy-done.5, ...), custom_call_target="tpu_custom_call" | custom-call | tf_op jit(solution)/shard_map/solve/pallas_call | solution.py:265
  33.6 16.3 %all_to_all.11.got = bf16[128,4,384]{2,1,0:T(4,128)(2,1)S(1)} all-to-all(bf16[128,4,384]{2,1,0:T(4,128)(2,1)S(1)} %solve.1), channel_id=1, replica_groups=mesh['sector_0'=4,'sector_1'=4,'sector_2'=2,'sector_3'=2,'dof'=2] {'sect..., dimensions={0} | all-to-all | bytes 786432 | tf_op jit(solution)/shard_map/all_to_all | solution.py:426
  49.9 0.0 copy-done.7
  49.9 5.1 %recover.1 = (f32[128,256]{1,0:T(8,128)}, bf16[128,16384]{1,0:T(8,128)(2,1)}, f32[16384,128]{1,0:T(8,128)S(1)}) custom-call(s32[512]{0:T(512)S(1)} %copy-done.7, s32[512]{0:T(512)S(1)} %copy-done.8, bf16[128,4,384]{2,1,0:T(4,128)(2,1)S(1)} %all_to_all.11.got, bf16[256,256]{1,0:T(8,128)(2,1)S(1)} %copy-done.1, ...), custom_call_target="tpu_custom_call", output_to_operand_aliasing={{2}: (6, {})} | custom-call | tf_op jit(solution)/shard_map/recover/pallas_call | solution.py:396
  (3 shorter events, 0.0 us)
Async XLA Ops:
  1.3 31.5 %copy-start = (bf16[512,256]{1,0:T(8,128)(2,1)S(1)}, bf16[512,256]{1,0:T(8,128)(2,1)}, u32[]{:S(2)}) copy-start(bf16[512,256]{1,0:T(8,128)(2,1)} %constant.19.clone.order) | copy-start | bytes 786436
  1.3 31.5 %copy-start.2 = (f32[64,512]{1,0:T(8,128)S(1)}, f32[64,512]{1,0:T(8,128)}, u32[]{:S(2)}) copy-start(f32[64,512]{1,0:T(8,128)} %eigen.1) | copy-start | bytes 393220
  1.3 31.5 %copy-start.3 = (bf16[128,256]{1,0:T(8,128)(2,1)S(1)}, bf16[128,256]{1,0:T(8,128)(2,1)}, u32[]{:S(2)}) copy-start(bf16[128,256]{1,0:T(8,128)(2,1)} %constant.16.clone.fwd_lo) | copy-start | bytes 196612
  1.3 31.5 %copy-start.4 = (bf16[128,256]{1,0:T(8,128)(2,1)S(1)}, bf16[128,256]{1,0:T(8,128)(2,1)}, u32[]{:S(2)}) copy-start(bf16[128,256]{1,0:T(8,128)(2,1)} %constant.15.clone.fwd_hi) | copy-start | bytes 196612
  1.3 31.5 %copy-start.5 = (bf16[128,128]{1,0:T(8,128)(2,1)S(1)}, bf16[128,128]{1,0:T(8,128)(2,1)}, u32[]{:S(2)}) copy-start(bf16[128,128]{1,0:T(8,128)(2,1)} %constant.18.clone.inv_lo) | copy-start | bytes 98308
  1.3 31.5 %copy-start.6 = (bf16[128,128]{1,0:T(8,128)(2,1)S(1)}, bf16[128,128]{1,0:T(8,128)(2,1)}, u32[]{:S(2)}) copy-start(bf16[128,128]{1,0:T(8,128)(2,1)} %constant.17.clone.inv_hi) | copy-start | bytes 98308
  1.4 31.5 %copy-start.9 = (f32[512]{0:T(512)S(1)}, f32[512]{0:T(512)}, u32[]{:S(2)}) copy-start(f32[512]{0:T(512)} %param.23) | copy-start | bytes 6148
  1.4 31.5 %copy-start.10 = (f32[64]{0:T(128)S(1)}, f32[64]{0:T(128)}, u32[]{:S(2)}) copy-start(f32[64]{0:T(128)} %param.24) | copy-start | bytes 772
  1.4 48.5 %copy-start.1 = (bf16[256,256]{1,0:T(8,128)(2,1)S(1)}, bf16[256,256]{1,0:T(8,128)(2,1)}, u32[]{:S(2)}) copy-start(bf16[256,256]{1,0:T(8,128)(2,1)} %constant.20.clone.order) | copy-start | bytes 393220
  1.4 48.5 %copy-start.7 = (s32[512]{0:T(512)S(1)}, s32[512]{0:T(512)}, u32[]{:S(2)}) copy-start(s32[512]{0:T(512)} %left_in.3) | copy-start | bytes 6148
  1.4 48.5 %copy-start.8 = (s32[512]{0:T(512)S(1)}, s32[512]{0:T(512)}, u32[]{:S(2)}) copy-start(s32[512]{0:T(512)} %right_in.3) | copy-start | bytes 6148

commit v2 on v1

--- a/solution.py
+++ b/solution.py
@@ -11,7 +11,7 @@
 from jax.sharding import PartitionSpec as P
 
 SECTOR = ("sector_0", "sector_1", "sector_2", "sector_3")
-EVERY = SECTOR + ("dof",)
+ROUTE = ("sector_3", "dof", "sector_2", "sector_1", "sector_0")
 BF16 = jnp.bfloat16
 F32 = jnp.float32
 EMPTY = 3.0e38
@@ -24,17 +24,22 @@
     return high, low
 
 
-def transforms(sectors, dofs):
+def sector_of_device(sizes):
+    places = np.unravel_index(np.arange(math.prod(sizes.values())), [sizes[a] for a in ROUTE])
+    places = dict(zip(ROUTE, places))
+    return np.ravel_multi_index([places[a] for a in SECTOR], [sizes[a] for a in SECTOR])
+
+
+def transforms(sectors, holders):
     turns = np.outer(np.arange(sectors), np.arange(sectors)) % sectors
     theta = turns * (2.0 * math.pi / sectors)
     cosine, sine = np.cos(theta), np.sin(theta)
-    forward = np.zeros((2, sectors, sectors, dofs, 2))
-    for d in range(dofs):
-        forward[0, :, :, d, 0] = cosine
-        forward[0, :, :, d, 1] = sine
-        forward[1, :, :, d, 0] = -sine
-        forward[1, :, :, d, 1] = cosine
-    forward = forward.reshape(2 * sectors, sectors * dofs * 2)
+    forward = np.zeros((2, sectors, holders.size, 2))
+    forward[0, :, :, 0] = cosine[:, holders]
+    forward[0, :, :, 1] = sine[:, holders]
+    forward[1, :, :, 0] = -sine[:, holders]
+    forward[1, :, :, 1] = cosine[:, holders]
+    forward = forward.reshape(2 * sectors, holders.size * 2)
     inverse = np.zeros((sectors, 2, 2, sectors))
     inverse[:, 0, 0, :] = cosine / sectors
     inverse[:, 0, 1, :] = -sine / sectors
@@ -56,10 +61,8 @@
     return pick((side * 2 + part) * freqs + f, 4 * freqs)
 
 
-def back_order(sectors, dofs):
-    s, _, part, lanes = np.meshgrid(
-        np.arange(sectors), np.arange(dofs), np.arange(2), np.arange(2), indexing="ij"
-    )
+def back_order(sectors, holders):
+    s, part, lanes = np.meshgrid(holders, np.arange(2), np.arange(2), indexing="ij")
     return pick(lanes * 2 * sectors + s * 2 + part, 4 * sectors)
 
 
@@ -234,7 +237,7 @@
 def solve_kernel(got, fwd_hi, fwd_lo, inv_hi, inv_lo, order, eigen, loss, omega_sq, out):
     sectors = eigen.shape[0]
     half = got.shape[-1]
-    me = lax.axis_index(EVERY)
+    me = lax.axis_index(ROUTE)
     side, freq = me % 2, me // 2
     rows = got[...].reshape(-1, half)
     spec = dot(fwd_hi[...], rows) + dot(fwd_lo[...], rows)
@@ -423,7 +426,7 @@
 
 
 def exchange(pieces):
-    return lax.all_to_all(pieces, EVERY, 0, 0, tiled=True)
+    return lax.all_to_all(pieces, ROUTE, 0, 0, tiled=True)
 
 
 def shards(
@@ -432,13 +435,13 @@
     rows = loads.shape[1]
     freqs = rows // 2
     sectors = lax.axis_size(SECTOR)
-    dofs = lax.axis_size("dof")
-    fwd, inv = transforms(sectors, dofs)
+    holders = sector_of_device({axis: lax.axis_size(axis) for axis in ROUTE})
+    fwd, inv = transforms(sectors, holders)
     sent, turned, near, spread = force(
         loads[0], modes, response[0], pattern, deviation, send_order(freqs), iface_left, iface_right
     )
     got = exchange(sent)
-    back = solve(got, fwd, inv, back_order(sectors, dofs), eigen, loss[None], omega_sq[None])
+    back = solve(got, fwd, inv, back_order(sectors, holders), eigen, loss[None], omega_sq[None])
     seen = exchange(back)
     modal, shown = recover(seen, seen_order(32), near, turned, spread, iface_left, iface_right)
     return modal[None], shown[None]

time: 55.2 us -> 54.6 us (0.989)
  blocking collectives: 37.7 us -> 37.1 us
where the time goes in v2:
time: 54.6 us; the launch traced here: 54.5 us
  blocking collectives  37.1 us (68%)
  Pallas kernels  15.8 us (29%)
  between operations  1.43 us (3%)
    all_to_all x2, blocking collectives, exchange(): return lax.all_to_all(pieces, ROUTE, 0, 0, tiled=True)  37.1 us
    pallas_call x1, Pallas kernels, force(): pl.pallas_call(force_kernel, out_shape=(pltpu.VMEM((rows, 2, half), BF16)...  9.93 us
    pallas_call x1, Pallas kernels, recover(): pl.pallas_call(recover_kernel, out_shape=(pltpu.HBM((rows, half), F32), p...  5.13 us

profile of v2, /device:TPU:1, one launch (start us, length us, event | category | flops | bytes accessed | tf_op | source)
XLA Modules:
  0.0 54.5 jit_solution(13133099520459293287)
XLA Ops:
  1.3 0.0 copy-start
  1.3 0.0 copy-start.2
  1.3 0.0 copy-start.3
  1.3 0.0 copy-start.4
  1.3 0.0 copy-start.5
  1.3 0.0 copy-start.6
  1.4 0.0 copy-start.9
  1.4 0.0 copy-start.10
  1.4 0.0 copy-start.1
  1.4 0.0 copy-start.7
  1.4 0.0 copy-start.8
  1.4 9.9 %force.1 = (bf16[128,2,256]{2,1,0:T(2,128)(2,1)S(1)}, bf16[512,16384]{1,0:T(8,128)(2,1)S(1)}, bf16[1024,512]{1,0:T(8,128)(2,1)S(1)}, f32[16384,128]{1,0:T(8,128)S(1)}) custom-call(s32[1]{0:T(128)S(6)} %copy.21.pattern, bf16[128,16384]{1,0:T(8,128)(2,1)} %bitcast.10, bf16[2048,8,512]{2,1,0:T(8,128)(2,1)} %bitcast.9, f32[128,256]{1,0:T(8,128)} %bitcast.11, ...), custom_call_target="tpu_custom_call" | custom-call | flops 2147483648 | bytes 20971520 | tf_op jit(solution)/shard_map/force/pallas_call | solution.py:201
  11.3 21.3 %all_to_all.10.got = bf16[128,2,256]{2,1,0:T(2,128)(2,1)S(1)} all-to-all(bf16[128,2,256]{2,1,0:T(2,128)(2,1)S(1)} %get-tuple-element.8), channel_id=1, replica_groups=mesh['sector_0'=4,'sector_1'=4,'sector_2'=2,'sector_3'=2,'dof'=2] {'sect..., dimensions={0} | all-to-all | bytes 262144 | tf_op jit(solution)/shard_map/all_to_all | solution.py:429
  32.6 0.0 copy-done
  32.6 0.0 copy-done.2
  32.7 0.0 copy-done.3
  32.7 0.0 copy-done.4
  32.7 0.0 copy-done.5
  32.7 0.0 copy-done.6
  32.7 0.0 copy-done.9
  32.7 0.8 %solve.1 = bf16[128,4,384]{2,1,0:T(4,128)(2,1)S(1)} custom-call(bf16[128,2,256]{2,1,0:T(2,128)(2,1)S(1)} %all_to_all.10.got, bf16[128,256]{1,0:T(8,128)(2,1)S(1)} %copy-done.4, bf16[128,256]{1,0:T(8,128)(2,1)S(1)} %copy-done.3, bf16[128,128]{1,0:T(8,128)(2,1)S(1)} %copy-done.6, bf16[128,128]{1,0:T(8,128)(2,1)S(1)} %copy-done.5, ...), custom_call_target="tpu_custom_call" | custom-call | tf_op jit(solution)/shard_map/solve/pallas_call | solution.py:268
  33.5 15.8 %all_to_all.11.got = bf16[128,4,384]{2,1,0:T(4,128)(2,1)S(1)} all-to-all(bf16[128,4,384]{2,1,0:T(4,128)(2,1)S(1)} %solve.1), channel_id=1, replica_groups=mesh['sector_0'=4,'sector_1'=4,'sector_2'=2,'sector_3'=2,'dof'=2] {'sect..., dimensions={0} | all-to-all | bytes 786432 | tf_op jit(solution)/shard_map/all_to_all | solution.py:429
  49.3 0.0 copy-done.1
  49.3 5.1 %recover.1 = (f32[128,256]{1,0:T(8,128)}, bf16[128,16384]{1,0:T(8,128)(2,1)}, f32[16384,128]{1,0:T(8,128)S(1)}) custom-call(s32[512]{0:T(512)S(1)} %copy-done.7, s32[512]{0:T(512)S(1)} %copy-done.8, bf16[128,4,384]{2,1,0:T(4,128)(2,1)S(1)} %all_to_all.11.got, bf16[256,256]{1,0:T(8,128)(2,1)S(1)} %copy-done.1, ...), custom_call_target="tpu_custom_call", output_to_operand_aliasing={{2}: (6, {})} | custom-call | tf_op jit(solution)/shard_map/recover/pallas_call | solution.py:399
  (3 shorter events, 0.0 us)
Async XLA Ops:
  1.3 31.4 %copy-start = (bf16[512,256]{1,0:T(8,128)(2,1)S(1)}, bf16[512,256]{1,0:T(8,128)(2,1)}, u32[]{:S(2)}) copy-start(bf16[512,256]{1,0:T(8,128)(2,1)} %constant.19.clone.order) | copy-start | bytes 786436
  1.3 31.4 %copy-start.2 = (f32[64,512]{1,0:T(8,128)S(1)}, f32[64,512]{1,0:T(8,128)}, u32[]{:S(2)}) copy-start(f32[64,512]{1,0:T(8,128)} %eigen.1) | copy-start | bytes 393220
  1.3 31.4 %copy-start.3 = (bf16[128,256]{1,0:T(8,128)(2,1)S(1)}, bf16[128,256]{1,0:T(8,128)(2,1)}, u32[]{:S(2)}) copy-start(bf16[128,256]{1,0:T(8,128)(2,1)} %constant.16.clone.fwd_lo) | copy-start | bytes 196612
  1.3 31.3 %copy-start.4 = (bf16[128,256]{1,0:T(8,128)(2,1)S(1)}, bf16[128,256]{1,0:T(8,128)(2,1)}, u32[]{:S(2)}) copy-start(bf16[128,256]{1,0:T(8,128)(2,1)} %constant.15.clone.fwd_hi) | copy-start | bytes 196612
  1.3 31.3 %copy-start.5 = (bf16[128,128]{1,0:T(8,128)(2,1)S(1)}, bf16[128,128]{1,0:T(8,128)(2,1)}, u32[]{:S(2)}) copy-start(bf16[128,128]{1,0:T(8,128)(2,1)} %constant.18.clone.inv_lo) | copy-start | bytes 98308
  1.3 31.3 %copy-start.6 = (bf16[128,128]{1,0:T(8,128)(2,1)S(1)}, bf16[128,128]{1,0:T(8,128)(2,1)}, u32[]{:S(2)}) copy-start(bf16[128,128]{1,0:T(8,128)(2,1)} %constant.17.clone.inv_hi) | copy-start | bytes 98308
  1.4 31.3 %copy-start.9 = (f32[512]{0:T(512)S(1)}, f32[512]{0:T(512)}, u32[]{:S(2)}) copy-start(f32[512]{0:T(512)} %param.23) | copy-start | bytes 6148
  1.4 31.3 %copy-start.10 = (f32[64]{0:T(128)S(1)}, f32[64]{0:T(128)}, u32[]{:S(2)}) copy-start(f32[64]{0:T(128)} %param.24) | copy-start | bytes 772
  1.4 47.9 %copy-start.1 = (bf16[256,256]{1,0:T(8,128)(2,1)S(1)}, bf16[256,256]{1,0:T(8,128)(2,1)}, u32[]{:S(2)}) copy-start(bf16[256,256]{1,0:T(8,128)(2,1)} %constant.20.clone.order) | copy-start | bytes 393220
  1.4 47.9 %copy-start.7 = (s32[512]{0:T(512)S(1)}, s32[512]{0:T(512)}, u32[]{:S(2)}) copy-start(s32[512]{0:T(512)} %left_in.3) | copy-start | bytes 6148
  1.4 47.9 %copy-start.8 = (s32[512]{0:T(512)S(1)}, s32[512]{0:T(512)}, u32[]{:S(2)}) copy-start(s32[512]{0:T(512)} %right_in.3) | copy-start | bytes 6148

commit v3 on v2

--- a/solution.py
+++ b/solution.py
@@ -93,8 +93,10 @@
     return pltpu.CompilerParams(vmem_limit_bytes=mib << 20)
 
 
-AHEAD = 6
-SLOTS = 8
+AHEAD = 4
+SLOTS = 5
+BLOCK = 1024
+LONG = 2 * BLOCK
 GROUP = 32
 ROWS = 8
 
@@ -131,8 +133,7 @@
 ):
     width = modes.shape[2]
     depth = modes.shape[0] * ROWS
-    block = depth // mode_sems.shape[0]
-    steps = depth // block
+    longs = depth // LONG - 1
     others = [
         pltpu.make_async_copy(response, acted, other_sems.at[0]),
         pltpu.make_async_copy(deviation, table, other_sems.at[1]),
@@ -141,13 +142,21 @@
         pltpu.make_async_copy(right_in, right, other_sems.at[4]),
     ]
 
-    def copies(k):
-        cut = part_of(k, block)
-        blocks = part_of(k, block // ROWS)
+    def copies(k, short=False):
+        span = BLOCK if short else LONG
+        place = (k + longs) if short else k
+        first = (longs * 2 + k) if short else k
+        slot = lax.rem(place, SLOTS)
         return (
-            pltpu.make_async_copy(modes.at[blocks], held.at[blocks], mode_sems.at[k]),
             pltpu.make_async_copy(
-                loads.at[:, cut], brought.at[lax.rem(k, SLOTS)], load_sems.at[k]
+                modes.at[part_of(first, span // ROWS)],
+                held.at[part_of(first, span // ROWS)],
+                mode_sems.at[place],
+            ),
+            pltpu.make_async_copy(
+                loads.at[:, part_of(first, span)],
+                brought.at[slot, :, pl.ds(0, span)],
+                load_sems.at[place],
             ),
         )
 
@@ -159,24 +168,41 @@
     total[...] = jnp.zeros_like(total)
     size = 256
 
+    def use(block, slot, at):
+        blocks = held[part_of(block, BLOCK // ROWS)].reshape(BLOCK, width)
+        total[...] += dot(brought[slot, :, at : at + BLOCK], blocks)
+        for j in range(BLOCK // size):
+            piece = block * (BLOCK // size) + j
+            here = part_of(piece, size)
+            turned[:, here] = held[part_of(piece, size // ROWS)].reshape(size, width).T
+            spread[here, :] = jnp.full((size, spread.shape[1]), EMPTY, F32)
+
     def step(k, carry):
         for c in copies(k):
             c.wait()
 
-        @pl.when(k + AHEAD < steps)
+        @pl.when(k + AHEAD < longs)
         def _():
             for c in copies(k + AHEAD):
                 c.start()
 
-        blocks = held[part_of(k, block // ROWS)].reshape(block, width)
-        total[...] += dot(brought[lax.rem(k, SLOTS)], blocks)
-        for j in range(block // size):
-            here = part_of(k * (block // size) + j, size)
-            turned[:, here] = held[part_of(k * (block // size) + j, size // ROWS)].reshape(size, width).T
-            spread[here, :] = jnp.full((size, spread.shape[1]), EMPTY, F32)
+        for short in range(2):
+
+            @pl.when(k + AHEAD == longs + short)
+            def _(short=short):
+                for c in copies(short, True):
+                    c.start()
+
+        slot = lax.rem(k, SLOTS)
+        for i in range(LONG // BLOCK):
+            use(k * (LONG // BLOCK) + i, slot, i * BLOCK)
         return carry
 
-    lax.fori_loop(0, steps, step, 0)
+    lax.fori_loop(0, longs, step, 0)
+    for short in range(2):
+        for c in copies(short, True):
+            c.wait()
+        use(longs * 2 + short, (longs + short) % SLOTS, 0)
     for c in others:
         c.wait()
     half = acted.shape[1]
@@ -192,7 +218,7 @@
     rows, depth = loads.shape
     width = modes.shape[1]
     half = response.shape[1]
-    steps = 16
+    reads = depth // LONG + 1
     entries = left.shape[0]
     vmem = pl.BlockSpec(memory_space=pltpu.VMEM)
     hbm = pl.BlockSpec(memory_space=pltpu.HBM)
@@ -210,15 +236,15 @@
         out_specs=(vmem,) * 4,
         scratch_shapes=[
             pltpu.VMEM((depth // ROWS, ROWS, width), BF16),
-            pltpu.VMEM((SLOTS, rows, depth // steps), BF16),
+            pltpu.VMEM((SLOTS, rows, LONG), BF16),
             pltpu.VMEM((rows, width), F32),
             pltpu.VMEM((rows, half), F32),
             pltpu.VMEM(deviation.shape, F32),
             pltpu.VMEM(order.shape, BF16),
             pltpu.SMEM((entries,), jnp.int32),
             pltpu.SMEM((entries,), jnp.int32),
-            pltpu.SemaphoreType.DMA((steps,)),
-            pltpu.SemaphoreType.DMA((steps,)),
+            pltpu.SemaphoreType.DMA((reads,)),
+            pltpu.SemaphoreType.DMA((reads,)),
             pltpu.SemaphoreType.DMA((6,)),
         ],
         compiler_params=params(21),
@@ -275,7 +301,7 @@
     )(*args)
 
 
-PHASES = (6144, 4096, 4096, 2048)
+PHASES = (5120, 4096, 4096, 2048, 1024)
 PIECE = 1024
 
 

time: 54.6 us -> 54.7 us (level)
  no operation moved by 1% of the time
where the time goes in v3:
time: 54.7 us; the launch traced here: 54.5 us
  blocking collectives  37.2 us (68%)
  Pallas kernels  15.9 us (29%)
  between operations  1.43 us (3%)
    all_to_all x2, blocking collectives, exchange(): return lax.all_to_all(pieces, ROUTE, 0, 0, tiled=True)  37.2 us
    pallas_call x1, Pallas kernels, force(): pl.pallas_call(force_kernel, out_shape=(pltpu.VMEM((rows, 2, half), BF16)...  10.1 us
    pallas_call x1, Pallas kernels, recover(): pl.pallas_call(recover_kernel, out_shape=(pltpu.HBM((rows, half), F32), p...  5.04 us

profile of v3, /device:TPU:1, one launch (start us, length us, event | category | flops | bytes accessed | tf_op | source)
XLA Modules:
  0.0 54.5 jit_solution(13012377491304824553)
XLA Ops:
  1.3 0.0 copy-start
  1.3 0.0 copy-start.2
  1.3 0.0 copy-start.3
  1.3 0.0 copy-start.4
  1.3 0.0 copy-start.5
  1.3 0.0 copy-start.6
  1.4 0.0 copy-start.9
  1.4 0.0 copy-start.10
  1.4 0.0 copy-start.1
  1.4 0.0 copy-start.7
  1.4 0.0 copy-start.8
  1.4 10.1 %force.1 = (bf16[128,2,256]{2,1,0:T(2,128)(2,1)S(1)}, bf16[512,16384]{1,0:T(8,128)(2,1)S(1)}, bf16[1024,512]{1,0:T(8,128)(2,1)S(1)}, f32[16384,128]{1,0:T(8,128)S(1)}) custom-call(s32[1]{0:T(128)S(6)} %copy.21.pattern, bf16[128,16384]{1,0:T(8,128)(2,1)} %bitcast.10, bf16[2048,8,512]{2,1,0:T(8,128)(2,1)} %bitcast.9, f32[128,256]{1,0:T(8,128)} %bitcast.11, ...), custom_call_target="tpu_custom_call" | custom-call | flops 2147483648 | bytes 20971520 | tf_op jit(solution)/shard_map/force/pallas_call | solution.py:227
  11.5 21.3 %all_to_all.10.got = bf16[128,2,256]{2,1,0:T(2,128)(2,1)S(1)} all-to-all(bf16[128,2,256]{2,1,0:T(2,128)(2,1)S(1)} %get-tuple-element.8), channel_id=1, replica_groups=mesh['sector_0'=4,'sector_1'=4,'sector_2'=2,'sector_3'=2,'dof'=2] {'sect..., dimensions={0} | all-to-all | bytes 262144 | tf_op jit(solution)/shard_map/all_to_all | solution.py:455
  32.8 0.0 copy-done
  32.8 0.0 copy-done.2
  32.8 0.0 copy-done.3
  32.8 0.0 copy-done.4
  32.8 0.0 copy-done.5
  32.8 0.0 copy-done.6
  32.9 0.0 copy-done.9
  32.9 0.8 %solve.1 = bf16[128,4,384]{2,1,0:T(4,128)(2,1)S(1)} custom-call(bf16[128,2,256]{2,1,0:T(2,128)(2,1)S(1)} %all_to_all.10.got, bf16[128,256]{1,0:T(8,128)(2,1)S(1)} %copy-done.4, bf16[128,256]{1,0:T(8,128)(2,1)S(1)} %copy-done.3, bf16[128,128]{1,0:T(8,128)(2,1)S(1)} %copy-done.6, bf16[128,128]{1,0:T(8,128)(2,1)S(1)} %copy-done.5, ...), custom_call_target="tpu_custom_call" | custom-call | tf_op jit(solution)/shard_map/solve/pallas_call | solution.py:294
  33.6 15.8 %all_to_all.11.got = bf16[128,4,384]{2,1,0:T(4,128)(2,1)S(1)} all-to-all(bf16[128,4,384]{2,1,0:T(4,128)(2,1)S(1)} %solve.1), channel_id=1, replica_groups=mesh['sector_0'=4,'sector_1'=4,'sector_2'=2,'sector_3'=2,'dof'=2] {'sect..., dimensions={0} | all-to-all | bytes 786432 | tf_op jit(solution)/shard_map/all_to_all | solution.py:455
  49.5 0.0 copy-done.8
  49.5 5.0 %recover.1 = (f32[128,256]{1,0:T(8,128)}, bf16[128,16384]{1,0:T(8,128)(2,1)}, f32[16384,128]{1,0:T(8,128)S(1)}) custom-call(s32[512]{0:T(512)S(1)} %copy-done.7, s32[512]{0:T(512)S(1)} %copy-done.8, bf16[128,4,384]{2,1,0:T(4,128)(2,1)S(1)} %all_to_all.11.got, bf16[256,256]{1,0:T(8,128)(2,1)S(1)} %copy-done.1, ...), custom_call_target="tpu_custom_call", output_to_operand_aliasing={{2}: (6, {})} | custom-call | tf_op jit(solution)/shard_map/recover/pallas_call | solution.py:425
  (3 shorter events, 0.0 us)
Async XLA Ops:
  1.3 31.5 %copy-start = (bf16[512,256]{1,0:T(8,128)(2,1)S(1)}, bf16[512,256]{1,0:T(8,128)(2,1)}, u32[]{:S(2)}) copy-start(bf16[512,256]{1,0:T(8,128)(2,1)} %constant.19.clone.order) | copy-start | bytes 786436
  1.3 31.5 %copy-start.2 = (f32[64,512]{1,0:T(8,128)S(1)}, f32[64,512]{1,0:T(8,128)}, u32[]{:S(2)}) copy-start(f32[64,512]{1,0:T(8,128)} %eigen.1) | copy-start | bytes 393220
  1.3 31.5 %copy-start.3 = (bf16[128,256]{1,0:T(8,128)(2,1)S(1)}, bf16[128,256]{1,0:T(8,128)(2,1)}, u32[]{:S(2)}) copy-start(bf16[128,256]{1,0:T(8,128)(2,1)} %constant.16.clone.fwd_lo) | copy-start | bytes 196612
  1.3 31.5 %copy-start.4 = (bf16[128,256]{1,0:T(8,128)(2,1)S(1)}, bf16[128,256]{1,0:T(8,128)(2,1)}, u32[]{:S(2)}) copy-start(bf16[128,256]{1,0:T(8,128)(2,1)} %constant.15.clone.fwd_hi) | copy-start | bytes 196612
  1.3 31.5 %copy-start.5 = (bf16[128,128]{1,0:T(8,128)(2,1)S(1)}, bf16[128,128]{1,0:T(8,128)(2,1)}, u32[]{:S(2)}) copy-start(bf16[128,128]{1,0:T(8,128)(2,1)} %constant.18.clone.inv_lo) | copy-start | bytes 98308
  1.3 31.5 %copy-start.6 = (bf16[128,128]{1,0:T(8,128)(2,1)S(1)}, bf16[128,128]{1,0:T(8,128)(2,1)}, u32[]{:S(2)}) copy-start(bf16[128,128]{1,0:T(8,128)(2,1)} %constant.17.clone.inv_hi) | copy-start | bytes 98308
  1.4 31.5 %copy-start.9 = (f32[512]{0:T(512)S(1)}, f32[512]{0:T(512)}, u32[]{:S(2)}) copy-start(f32[512]{0:T(512)} %param.23) | copy-start | bytes 6148
  1.4 31.5 %copy-start.10 = (f32[64]{0:T(128)S(1)}, f32[64]{0:T(128)}, u32[]{:S(2)}) copy-start(f32[64]{0:T(128)} %param.24) | copy-start | bytes 772
  1.4 48.1 %copy-start.1 = (bf16[256,256]{1,0:T(8,128)(2,1)S(1)}, bf16[256,256]{1,0:T(8,128)(2,1)}, u32[]{:S(2)}) copy-start(bf16[256,256]{1,0:T(8,128)(2,1)} %constant.20.clone.order) | copy-start | bytes 393220
  1.4 48.1 %copy-start.7 = (s32[512]{0:T(512)S(1)}, s32[512]{0:T(512)}, u32[]{:S(2)}) copy-start(s32[512]{0:T(512)} %left_in.3) | copy-start | bytes 6148
  1.4 48.1 %copy-start.8 = (s32[512]{0:T(512)S(1)}, s32[512]{0:T(512)}, u32[]{:S(2)}) copy-start(s32[512]{0:T(512)} %right_in.3) | copy-start | bytes 6148
